TPU v7x, 256 devices: a whole 4x4x8 slice. The times are simulated.
256 devices in a mesh: days: 128 (over x, z, y), cols: 2 (over core).
Axes of the slice: x: 4, y: 4, z: 8, core: 2. Of those that a mesh axis runs over, the one named last changes fastest.
Arguments:
- cube: float32 [4096, 65536], P('days', 'cols'), may hold values from -800 to 800
- year_id: int32 [4096], P('days'), may hold values from 0 to 2, as said below
- parent: int32 [65536], P('cols'), may hold values from 0 to 511
Outputs:
- running: float32 [4096, 65536], P('days', 'cols')
- rollup: float32 [4096, 512], P('days', 'cols')
Inputs may be any that keep to these rules, and one draw needn't show every extreme that they name: year_id never falls from one day to the next; every year of 0 to 2 has 1 to 3072 days.
All inputs are finite; a program needn't handle non-finite values.
Results may differ from a plain program's by a relative error of at most 0.00012.
Values sent between devices are 32-bit elements; how exact they have to be, the bound alone decides.
A program may use at most 128 MiB of HBM per device.

v0:
```python
import math
import jax
import jax.numpy as jnp
from jax import lax
from jax.sharding import Mesh
from jax.sharding import PartitionSpec as P

PARENTS = 512
DAYS = ("days_0", "days_1", "days_2")


def side_by_side(arrays, axis, dim, along):
    widths = [math.prod(a.shape[along:]) for a in arrays]
    both = jnp.concatenate(
        [a.reshape(*a.shape[:along], w) for a, w in zip(arrays, widths)], axis=along
    )
    out = lax.all_gather(both, axis, axis=dim, tiled=True)
    tiles = jnp.split(out, [sum(widths[:k]) for k in range(1, len(widths))], axis=along)
    return tuple((b.reshape(*out.shape[:along], *a.shape[along:]) for a, b in zip(arrays, tiles)))


def from_everyone(array, axis):
    peers = lax.axis_size(axis)
    return lax.all_to_all(
        jnp.broadcast_to(array[None], (peers, *array.shape)), axis, 0, 0, tiled=True
    )


def over_copies(array, axis):
    everything = from_everyone(array, axis)
    return jnp.sum(everything, axis=0)


def one_axis_at_a_time(array, axes):
    for axis in axes:
        array = lax.psum(array, axis)
    return array


def parent_totals(ytd, parent):
    width = ytd.shape[1]
    block = min(width, 4096)
    nblocks = width // block
    targets = jnp.arange(PARENTS, dtype=jnp.int32)

    def add_block(index, total):
        begin = (index * block).astype(jnp.int32)
        rows = lax.dynamic_slice_in_dim(ytd, begin, block, 1)
        owners = lax.dynamic_slice_in_dim(parent, begin, block, 0)
        onehot = (owners[:, None] == targets[None, :]).astype(jnp.float32)
        return total + jnp.dot(
            rows, onehot, preferred_element_type=jnp.float32, precision=lax.Precision.HIGHEST
        )

    start = jnp.zeros((ytd.shape[0], PARENTS), jnp.float32)
    return lax.fori_loop(0, nblocks, add_block, start)


def body(cube, year_id, parent):
    day_count = cube.shape[0]
    years = year_id.astype(jnp.float32)
    order = jnp.arange(day_count, dtype=jnp.int32)
    lower = jnp.logical_and(order[None, :] <= order[:, None], years[None, :] == years[:, None])
    local = jnp.dot(
        lower.astype(jnp.float32),
        cube,
        preferred_element_type=jnp.float32,
        precision=lax.Precision.HIGHEST,
    )
    first = years[:1]
    last = years[-1:]
    tail = local[-1]
    mine = lax.axis_index(DAYS)
    lasts, tails = side_by_side((last, tail[None, :]), DAYS, 0, 1)
    index = jnp.arange(lasts.shape[0], dtype=jnp.int32)
    weights = jnp.logical_and(index < mine, lasts == first[0]).astype(jnp.float32)
    carried = jnp.dot(
        weights[None, :], tails, preferred_element_type=jnp.float32, precision=lax.Precision.HIGHEST
    )[0]
    ytd = local + jnp.where(years[:, None] == first[0], carried[None, :], 0.0)
    partial_region = parent_totals(ytd, parent)
    total_days = day_count * lax.axis_size(DAYS)
    whole = over_copies(partial_region, "cols")
    squares = one_axis_at_a_time(jnp.sum(whole * whole), DAYS)
    share = PARENTS // lax.axis_size("cols")
    region = lax.dynamic_slice_in_dim(whole, lax.axis_index("cols") * share, share, 1)
    scale = jnp.sqrt(squares / (total_days * PARENTS) + 1e-06)
    return (ytd / scale, region / scale)


def solution(mesh):
    finer = Mesh(
        mesh.devices.reshape(4, 8, 4, mesh.shape["cols"]), ("days_0", "days_1", "days_2", "cols")
    )
    return jax.shard_map(
        body,
        mesh=finer,
        in_specs=(P(DAYS, "cols"), P(DAYS), P("cols")),
        out_specs=(P(DAYS, "cols"), P(DAYS, "cols")),
        check_vma=False,
    )
```

profile of v0, /device:TPU:2, one launch (start us, length us, event | category | flops | bytes accessed | tf_op | source)
XLA Modules:
  0.0 313.8 jit_solution(10033284970401329339)
XLA Ops:
  7.2 0.0 all-gather.3.cloned.1.call-start
  7.2 0.7 convert_element_type.8
  7.9 0.6 fusion.22
  8.5 0.0 copy-start.2
  8.5 4.5 %fusion.10 = f32[32,32768]{1,0:T(8,128)S(1)} fusion(f32[32,32768]{1,0:T(8,128)} %param.5, f32[32]{0:T(128)S(1)} %convert_element_type.8), kind=kOutput, calls=%fused_computation.16 | convolution fusion | flops 402656256 | bytes 8388736 | tf_op jit(solution)/shard_map/dot_general | solution.py:64
  12.9 0.0 copy-start
  12.9 2.0 copy-done
  14.9 0.1 slice.12
  15.1 1.6 maximum_bitcast_fusion
  16.7 0.0 all-gather.3.cloned.1.call-update
  16.8 0.0 copy-done.2
  16.8 0.6 broadcast_compare_fusion
  17.4 152.5 %all-gather.3.cloned.1.call-done = f32[128,1,32769]{2,1,0:T(1,128)} async-done(((f32[1,1,32769]{2,1,0:T(1,128)}), f32[128,1,32769]{2,1,0:T(1,128)}) %all-gather.3.cloned.1.call-update) | async-done | bytes 16777744 | tf_op jit(solution)/shard_map/all_gather | solution.py:17
  169.9 34.6 %copy.7 = f32[128,1,32769]{0,2,1:T(8,128)} copy(f32[128,1,32769]{2,1,0:T(1,128)} %all-gather.3.cloned.1.call-done) | data formatting | bytes 33555456 | tf_op jit(solution)/shard_map/all_gather | solution.py:17
  204.5 0.0 copy-start.1
  204.5 14.8 %fusion.7 = f32[1,32768]{1,0:T(1,128)S(1)} fusion(f32[128,32769]{0,1:T(8,128)} %bitcast.15, f32[]{:T(128)} %bitcast, s32[]{:T(128)S(6)} %add.53), kind=kOutput, calls=%fused_computation.7 | convolution fusion | flops 50332032 | bytes 16909316 | tf_op jit(solution)/shard_map/dot_general | solution.py:77
  219.3 0.0 copy-done.1
  219.3 2.4 select_add_fusion
  221.7 38.6 %while.14 = (s32[]{:T(128)}, f32[32,512]{1,0:T(8,128)S(1)}, f32[32,32768]{1,0:T(8,128)}, s32[32768]{0:T(1024)}, s32[]{:T(128)}, /*index=5*/s32[]{:T(128)}, s32[]{:T(128)}, s32[]{:T(128)}) while((s32[]{:T(128)}, f32[32,512]{1,0:T(8,128)S(1)}, f32[32,32768]{1,0:T(8,128)}, s32[32768]{0:T(1024)}, s32[]{:T(128)}, /*index=5*/s32[]{:T(128)}, ...), condition=%wide.region_1.2_spmd.clone, body=%wide.region_0.1_spmd.clone.sunk | while | flops 807436288 | bytes 704661 | solution.py:56
  221.7 0.7 dynamic_slice.26
  222.4 4.1 %fusion.27 = f32[32,512]{1,0:T(8,128)S(1)} fusion(s32[4096]{0:T(1024)S(1)} %dynamic_slice.26, f32[32,32768]{1,0:T(8,128)} %get-tuple-element.167, s32[]{:T(128)S(6)} %select_n.22, f32[32,512]{1,0:T(8,128)S(1)} %get-tuple-element.158, pred[]{:T(512)S(6)} %compare.3), kind=kOutput, calls=%fused_computation.4.clone.1 | convolution fusion | flops 807436288 | bytes 671749 | tf_op jit(solution)/shard_map/while/body/eval_jaxpr/dot_general | solution.py:51
  226.5 0.7 dynamic_slice.26
  227.3 4.1 %fusion.27 = f32[32,512]{1,0:T(8,128)S(1)} fusion(s32[4096]{0:T(1024)S(1)} %dynamic_slice.26, f32[32,32768]{1,0:T(8,128)} %get-tuple-element.167, s32[]{:T(128)S(6)} %select_n.22, f32[32,512]{1,0:T(8,128)S(1)} %get-tuple-element.158, pred[]{:T(512)S(6)} %compare.3), kind=kOutput, calls=%fused_computation.4.clone.1 | convolution fusion | flops 807436288 | bytes 671749 | tf_op jit(solution)/shard_map/while/body/eval_jaxpr/dot_general | solution.py:51
  231.4 0.7 dynamic_slice.26
  232.1 4.1 %fusion.27 = f32[32,512]{1,0:T(8,128)S(1)} fusion(s32[4096]{0:T(1024)S(1)} %dynamic_slice.26, f32[32,32768]{1,0:T(8,128)} %get-tuple-element.167, s32[]{:T(128)S(6)} %select_n.22, f32[32,512]{1,0:T(8,128)S(1)} %get-tuple-element.158, pred[]{:T(512)S(6)} %compare.3), kind=kOutput, calls=%fused_computation.4.clone.1 | convolution fusion | flops 807436288 | bytes 671749 | tf_op jit(solution)/shard_map/while/body/eval_jaxpr/dot_general | solution.py:51
  236.2 0.7 dynamic_slice.26
  236.9 4.1 %fusion.27 = f32[32,512]{1,0:T(8,128)S(1)} fusion(s32[4096]{0:T(1024)S(1)} %dynamic_slice.26, f32[32,32768]{1,0:T(8,128)} %get-tuple-element.167, s32[]{:T(128)S(6)} %select_n.22, f32[32,512]{1,0:T(8,128)S(1)} %get-tuple-element.158, pred[]{:T(512)S(6)} %compare.3), kind=kOutput, calls=%fused_computation.4.clone.1 | convolution fusion | flops 807436288 | bytes 671749 | tf_op jit(solution)/shard_map/while/body/eval_jaxpr/dot_general | solution.py:51
  241.0 0.7 dynamic_slice.26
  241.8 4.1 %fusion.27 = f32[32,512]{1,0:T(8,128)S(1)} fusion(s32[4096]{0:T(1024)S(1)} %dynamic_slice.26, f32[32,32768]{1,0:T(8,128)} %get-tuple-element.167, s32[]{:T(128)S(6)} %select_n.22, f32[32,512]{1,0:T(8,128)S(1)} %get-tuple-element.158, pred[]{:T(512)S(6)} %compare.3), kind=kOutput, calls=%fused_computation.4.clone.1 | convolution fusion | flops 807436288 | bytes 671749 | tf_op jit(solution)/shard_map/while/body/eval_jaxpr/dot_general | solution.py:51
  245.9 0.7 dynamic_slice.26
  246.6 4.1 %fusion.27 = f32[32,512]{1,0:T(8,128)S(1)} fusion(s32[4096]{0:T(1024)S(1)} %dynamic_slice.26, f32[32,32768]{1,0:T(8,128)} %get-tuple-element.167, s32[]{:T(128)S(6)} %select_n.22, f32[32,512]{1,0:T(8,128)S(1)} %get-tuple-element.158, pred[]{:T(512)S(6)} %compare.3), kind=kOutput, calls=%fused_computation.4.clone.1 | convolution fusion | flops 807436288 | bytes 671749 | tf_op jit(solution)/shard_map/while/body/eval_jaxpr/dot_general | solution.py:51
  250.7 0.7 dynamic_slice.26
  251.4 4.1 %fusion.27 = f32[32,512]{1,0:T(8,128)S(1)} fusion(s32[4096]{0:T(1024)S(1)} %dynamic_slice.26, f32[32,32768]{1,0:T(8,128)} %get-tuple-element.167, s32[]{:T(128)S(6)} %select_n.22, f32[32,512]{1,0:T(8,128)S(1)} %get-tuple-element.158, pred[]{:T(512)S(6)} %compare.3), kind=kOutput, calls=%fused_computation.4.clone.1 | convolution fusion | flops 807436288 | bytes 671749 | tf_op jit(solution)/shard_map/while/body/eval_jaxpr/dot_general | solution.py:51
  255.5 0.7 dynamic_slice.26
  256.3 4.1 %fusion.27 = f32[32,512]{1,0:T(8,128)S(1)} fusion(s32[4096]{0:T(1024)S(1)} %dynamic_slice.26, f32[32,32768]{1,0:T(8,128)} %get-tuple-element.167, s32[]{:T(128)S(6)} %select_n.22, f32[32,512]{1,0:T(8,128)S(1)} %get-tuple-element.158, pred[]{:T(512)S(6)} %compare.3), kind=kOutput, calls=%fused_computation.4.clone.1 | convolution fusion | flops 807436288 | bytes 671749 | tf_op jit(solution)/shard_map/while/body/eval_jaxpr/dot_general | solution.py:51
  260.4 3.8 %all_to_all.5 = f32[2,32,512]{2,1,0:T(8,128)S(1)} all-to-all(f32[2,32,512]{2,1,0:T(8,128)S(1)} %broadcast_in_dim.45), channel_id=1, replica_groups=mesh['days_0'=4,'days_1'=8,'days_2'=4,'cols'=2] {'cols'}, dimensions={0} | all-to-all | bytes 262144 | tf_op jit(solution)/shard_map/all_to_all | solution.py:24
  264.2 0.6 multiply_reduce_fusion
  264.8 9.2 %psum.21 = f32[]{:T(128)} all-reduce(f32[]{:T(128)} %multiply_reduce_fusion), channel_id=1, replica_groups=mesh['days_0'=4,'days_1'=8,'days_2'=4,'cols'=2] {'days_0'}, use_global_device_ids=true, to_apply=%region_4.5 | all-reduce | flops 1 | bytes 8 | tf_op jit(solution)/shard_map/psum | solution.py:36
  274.0 16.1 %psum.22 = f32[]{:T(128)} all-reduce(f32[]{:T(128)} %psum.21), channel_id=1, replica_groups=mesh['days_0'=4,'days_1'=8,'days_2'=4,'cols'=2] {'days_1'}, use_global_device_ids=true, to_apply=%region_5.6 | all-reduce | flops 1 | bytes 8 | tf_op jit(solution)/shard_map/psum | solution.py:36
  290.2 10.8 %psum.23 = f32[]{:T(128)} all-reduce(f32[]{:T(128)} %psum.22), channel_id=1, replica_groups=mesh['days_0'=4,'days_1'=8,'days_2'=4,'cols'=2] {'days_2'}, use_global_device_ids=true, to_apply=%region_6.7 | all-reduce | flops 1 | bytes 8 | tf_op jit(solution)/shard_map/psum | solution.py:36
  301.6 4.7 %broadcast_divide_fusion = f32[32,32768]{1,0:T(8,128)} fusion(f32[]{:T(128)S(6)} %sqrt.3, f32[32,32768]{1,0:T(8,128)} %copy-done, f32[32768]{0:T(1024)S(1)} %bitcast.17, pred[32]{0:T(512)(128)(4,1)S(1)} %broadcast_compare_fusion), kind=kLoop, calls=%fused_computation.10 | loop fusion | flops 3145728 | bytes 8519716 | tf_op jit(solution)/shard_map/div | solution.py:88
  306.3 0.6 dynamic-slice_divide_fusion
  (3 shorter events, 0.0 us)
Async XLA Ops:
  7.2 162.7 %all-gather.3.cloned.1.call-start = ((), (), s32[]{:S(2)}) async-start(), calls=%async_computation.1 | async-start | bytes 16974336 | tf_op jit(solution)/shard_map/all_gather | solution.py:17
  8.5 8.3 %copy-start.2 = (s32[32]{0:T(128)S(1)}, s32[32]{0:T(128)}, u32[]{:S(2)}) copy-start(s32[32]{0:T(128)} %param.6) | copy-start | bytes 388
  12.9 2.0 copy-start
  204.5 14.8 %copy-start.1 = (f32[32,32768]{1,0:T(8,128)S(1)}, f32[32,32768]{1,0:T(8,128)}, u32[]{:S(2)}) copy-start(f32[32,32768]{1,0:T(8,128)} %copy-done) | copy-start | bytes 12582916
Sparse Core Ops, SparseCore 0:
  16.8 152.9 all-gather.2
where the time goes:
time: 316 us; the launch traced here: 314 us
  waiting for transfers between devices  152 us (48%)
  matrix products  52 us (16%)
  local copies, waits for them, and re-layouts  43.1 us (14%)
  blocking collectives  39.9 us (13%)
  between operations  14.8 us (5%)
  other arithmetic  11.2 us (4%)
    all_gather x1, waiting for transfers between devices, side_by_side(): out = lax.all_gather(both, axis, axis=dim, tiled=True)  152 us
    psum x3, blocking collectives, one_axis_at_a_time(): array = lax.psum(array, axis)  36.1 us
    all_gather x1, local copies, waits for them, and re-layouts, side_by_side(): out = lax.all_gather(both, axis, axis=dim, tiled=True)  34.6 us
    dot_general x8, matrix products, add_block(): jnp.dot(rows, onehot, preferred_element_type=jnp.float32, precision=lax.P...  32.7 us
    dot_general x1, matrix products, body(): jnp.dot(weights[None, :], tails, preferred_element_type=jnp.float32, prec...  14.8 us
  transfers between devices with their start and end apart: 1, of which 1 were waited for; matrix products, arithmetic and copies ran while one was open for 0% of the time, Pallas kernels for 0%

commit v1 on v0

--- a/solution.py
+++ b/solution.py
@@ -33,7 +33,7 @@
 
 def one_axis_at_a_time(array, axes):
     for axis in axes:
-        array = lax.psum(array, axis)
+        array = jnp.sum(lax.all_gather(array, axis), axis=0)
     return array
 
 

time: 316 us -> 320 us (1.013)
  local copies, waits for them, and re-layouts: 43.1 us -> 49 us
    psum x3 -> x0, blocking collectives: 36.1 us -> none  [one_axis_at_a_time(): array = lax.psum(array, axis)]
    unnamed x0 -> x3, blocking collectives: none -> 34.2 us
    unnamed x6 -> x21, local copies, waits for them, and re-layouts: 2.02 us -> 7.84 us
  transfers between devices with their start and end apart: 1 -> 1, of which waited for: 1 -> 1; matrix products, arithmetic and copies ran while one was open for 0% -> 1% of each run, Pallas kernels for 0% -> 0%
where the time goes in v1:
time: 320 us; the launch traced here: 318 us
  waiting for transfers between devices  151 us (47%)
  matrix products  51.9 us (16%)
  local copies, waits for them, and re-layouts  49 us (15%)
  blocking collectives  38 us (12%)
  between operations  14.8 us (5%)
  other arithmetic  13 us (4%)
    all_gather x1, waiting for transfers between devices, side_by_side(): out = lax.all_gather(both, axis, axis=dim, tiled=True)  151 us
    all_gather x1, local copies, waits for them, and re-layouts, side_by_side(): out = lax.all_gather(both, axis, axis=dim, tiled=True)  34.6 us
    unnamed x3, blocking collectives  34.2 us
    dot_general x8, matrix products, add_block(): jnp.dot(rows, onehot, preferred_element_type=jnp.float32, precision=lax.P...  32.6 us
    dot_general x1, matrix products, body(): jnp.dot(weights[None, :], tails, preferred_element_type=jnp.float32, prec...  14.8 us
    unnamed x21, local copies, waits for them, and re-layouts  7.84 us
  transfers between devices with their start and end apart: 1, of which 1 were waited for; matrix products, arithmetic and copies ran while one was open for 1% of the time, Pallas kernels for 0%

profile of v1, /device:TPU:2, one launch (start us, length us, event | category | flops | bytes accessed | tf_op | source)
XLA Modules:
  0.0 317.7 jit_solution(806661797640924401)
XLA Ops:
  7.2 0.0 all-gather.3.cloned.1.call-start
  7.2 0.7 convert_element_type.8
  7.9 0.6 fusion.22
  8.5 4.5 %fusion.10 = f32[32,32768]{1,0:T(8,128)S(1)} fusion(f32[32,32768]{1,0:T(8,128)} %param.5, f32[32]{0:T(128)S(1)} %convert_element_type.8), kind=kOutput, calls=%fused_computation.16 | convolution fusion | flops 402656256 | bytes 8388736 | tf_op jit(solution)/shard_map/dot_general | solution.py:64
  13.0 0.0 copy-start
  13.0 2.0 copy-done
  15.0 0.1 slice.12
  15.1 1.6 maximum_bitcast_fusion
  16.7 0.0 all-gather.3.cloned.1.call-update
  16.8 0.0 copy-done.5
  16.8 0.6 dynamic-slice
  17.4 0.5 dynamic-slice.1
  18.0 0.6 dynamic-slice.2
  18.6 0.6 broadcast_compare_fusion
  19.1 150.8 %all-gather.3.cloned.1.call-done = f32[128,1,32769]{2,1,0:T(1,128)} async-done(((f32[1,1,32769]{2,1,0:T(1,128)}), f32[128,1,32769]{2,1,0:T(1,128)}) %all-gather.3.cloned.1.call-update) | async-done | bytes 16777744 | tf_op jit(solution)/shard_map/all_gather | solution.py:17
  169.9 34.6 %copy.7 = f32[128,1,32769]{0,2,1:T(8,128)} copy(f32[128,1,32769]{2,1,0:T(1,128)} %all-gather.3.cloned.1.call-done) | data formatting | bytes 33555456 | tf_op jit(solution)/shard_map/all_gather | solution.py:17
  204.6 14.8 %fusion.7 = f32[1,32768]{1,0:T(1,128)S(1)} fusion(f32[128,32769]{0,1:T(8,128)} %bitcast.21, f32[]{:T(128)} %bitcast, s32[]{:T(128)S(6)} %add.47), kind=kOutput, calls=%fused_computation.7 | convolution fusion | flops 50332032 | bytes 16909316 | tf_op jit(solution)/shard_map/dot_general | solution.py:77
  219.3 2.4 select_add_fusion
  221.7 38.6 %while.14 = (s32[]{:T(128)}, f32[32,512]{1,0:T(8,128)S(1)}, f32[32,32768]{1,0:T(8,128)}, s32[32768]{0:T(1024)}, s32[]{:T(128)}, /*index=5*/s32[]{:T(128)}, s32[]{:T(128)}, s32[]{:T(128)}) while((s32[]{:T(128)}, f32[32,512]{1,0:T(8,128)S(1)}, f32[32,32768]{1,0:T(8,128)}, s32[32768]{0:T(1024)}, s32[]{:T(128)}, /*index=5*/s32[]{:T(128)}, ...), condition=%wide.region_1.2_spmd.clone, body=%wide.region_0.1_spmd.clone.sunk | while | flops 807436288 | bytes 704661 | solution.py:56
  221.7 0.7 dynamic_slice.26
  222.4 4.1 %fusion.27 = f32[32,512]{1,0:T(8,128)S(1)} fusion(s32[4096]{0:T(1024)S(1)} %dynamic_slice.26, f32[32,32768]{1,0:T(8,128)} %get-tuple-element.167, s32[]{:T(128)S(6)} %select_n.22, f32[32,512]{1,0:T(8,128)S(1)} %get-tuple-element.158, pred[]{:T(512)S(6)} %compare.3), kind=kOutput, calls=%fused_computation.4.clone.1 | convolution fusion | flops 807436288 | bytes 671749 | tf_op jit(solution)/shard_map/while/body/eval_jaxpr/dot_general | solution.py:51
  226.5 0.7 dynamic_slice.26
  227.2 4.1 %fusion.27 = f32[32,512]{1,0:T(8,128)S(1)} fusion(s32[4096]{0:T(1024)S(1)} %dynamic_slice.26, f32[32,32768]{1,0:T(8,128)} %get-tuple-element.167, s32[]{:T(128)S(6)} %select_n.22, f32[32,512]{1,0:T(8,128)S(1)} %get-tuple-element.158, pred[]{:T(512)S(6)} %compare.3), kind=kOutput, calls=%fused_computation.4.clone.1 | convolution fusion | flops 807436288 | bytes 671749 | tf_op jit(solution)/shard_map/while/body/eval_jaxpr/dot_general | solution.py:51
  231.3 0.7 dynamic_slice.26
  232.1 4.1 %fusion.27 = f32[32,512]{1,0:T(8,128)S(1)} fusion(s32[4096]{0:T(1024)S(1)} %dynamic_slice.26, f32[32,32768]{1,0:T(8,128)} %get-tuple-element.167, s32[]{:T(128)S(6)} %select_n.22, f32[32,512]{1,0:T(8,128)S(1)} %get-tuple-element.158, pred[]{:T(512)S(6)} %compare.3), kind=kOutput, calls=%fused_computation.4.clone.1 | convolution fusion | flops 807436288 | bytes 671749 | tf_op jit(solution)/shard_map/while/body/eval_jaxpr/dot_general | solution.py:51
  236.2 0.7 dynamic_slice.26
  236.9 4.1 %fusion.27 = f32[32,512]{1,0:T(8,128)S(1)} fusion(s32[4096]{0:T(1024)S(1)} %dynamic_slice.26, f32[32,32768]{1,0:T(8,128)} %get-tuple-element.167, s32[]{:T(128)S(6)} %select_n.22, f32[32,512]{1,0:T(8,128)S(1)} %get-tuple-element.158, pred[]{:T(512)S(6)} %compare.3), kind=kOutput, calls=%fused_computation.4.clone.1 | convolution fusion | flops 807436288 | bytes 671749 | tf_op jit(solution)/shard_map/while/body/eval_jaxpr/dot_general | solution.py:51
  241.0 0.7 dynamic_slice.26
  241.7 4.1 %fusion.27 = f32[32,512]{1,0:T(8,128)S(1)} fusion(s32[4096]{0:T(1024)S(1)} %dynamic_slice.26, f32[32,32768]{1,0:T(8,128)} %get-tuple-element.167, s32[]{:T(128)S(6)} %select_n.22, f32[32,512]{1,0:T(8,128)S(1)} %get-tuple-element.158, pred[]{:T(512)S(6)} %compare.3), kind=kOutput, calls=%fused_computation.4.clone.1 | convolution fusion | flops 807436288 | bytes 671749 | tf_op jit(solution)/shard_map/while/body/eval_jaxpr/dot_general | solution.py:51
  245.8 0.7 dynamic_slice.26
  246.6 4.1 %fusion.27 = f32[32,512]{1,0:T(8,128)S(1)} fusion(s32[4096]{0:T(1024)S(1)} %dynamic_slice.26, f32[32,32768]{1,0:T(8,128)} %get-tuple-element.167, s32[]{:T(128)S(6)} %select_n.22, f32[32,512]{1,0:T(8,128)S(1)} %get-tuple-element.158, pred[]{:T(512)S(6)} %compare.3), kind=kOutput, calls=%fused_computation.4.clone.1 | convolution fusion | flops 807436288 | bytes 671749 | tf_op jit(solution)/shard_map/while/body/eval_jaxpr/dot_general | solution.py:51
  250.7 0.7 dynamic_slice.26
  251.4 4.1 %fusion.27 = f32[32,512]{1,0:T(8,128)S(1)} fusion(s32[4096]{0:T(1024)S(1)} %dynamic_slice.26, f32[32,32768]{1,0:T(8,128)} %get-tuple-element.167, s32[]{:T(128)S(6)} %select_n.22, f32[32,512]{1,0:T(8,128)S(1)} %get-tuple-element.158, pred[]{:T(512)S(6)} %compare.3), kind=kOutput, calls=%fused_computation.4.clone.1 | convolution fusion | flops 807436288 | bytes 671749 | tf_op jit(solution)/shard_map/while/body/eval_jaxpr/dot_general | solution.py:51
  255.5 0.7 dynamic_slice.26
  256.2 4.1 %fusion.27 = f32[32,512]{1,0:T(8,128)S(1)} fusion(s32[4096]{0:T(1024)S(1)} %dynamic_slice.26, f32[32,32768]{1,0:T(8,128)} %get-tuple-element.167, s32[]{:T(128)S(6)} %select_n.22, f32[32,512]{1,0:T(8,128)S(1)} %get-tuple-element.158, pred[]{:T(512)S(6)} %compare.3), kind=kOutput, calls=%fused_computation.4.clone.1 | convolution fusion | flops 807436288 | bytes 671749 | tf_op jit(solution)/shard_map/while/body/eval_jaxpr/dot_general | solution.py:51
  260.3 3.8 %all_to_all.5 = f32[2,32,512]{2,1,0:T(8,128)S(1)} all-to-all(f32[2,32,512]{2,1,0:T(8,128)S(1)} %broadcast_in_dim.45), channel_id=1, replica_groups=mesh['days_0'=4,'days_1'=8,'days_2'=4,'cols'=2] {'cols'}, dimensions={0} | all-to-all | bytes 262144 | tf_op jit(solution)/shard_map/all_to_all | solution.py:24
  264.2 0.6 multiply_reduce_fusion
  264.8 1.4 dynamic-update-slice
  266.2 8.6 %all-reduce = f32[4]{0:T(128)S(1)} all-reduce(f32[4]{0:T(128)S(1)} %dynamic-update-slice), channel_id=1, replica_groups=mesh['days_0'=4,'days_1'=8,'days_2'=4,'cols'=2] {'days_0'}, use_global_device_ids=true, to_apply=%add | all-reduce | flops 4 | bytes 32
  274.8 0.6 reduce_sum.47
  275.4 1.3 dynamic-update-slice.1
  276.7 15.5 %all-reduce.1 = f32[8]{0:T(128)S(1)} all-reduce(f32[8]{0:T(128)S(1)} %dynamic-update-slice.1), channel_id=1, replica_groups=mesh['days_0'=4,'days_1'=8,'days_2'=4,'cols'=2] {'days_1'}, use_global_device_ids=true, to_apply=%add.1 | all-reduce | flops 8 | bytes 64
  292.2 0.6 reduce_sum.48
  292.8 1.4 dynamic-update-slice.2
  294.1 10.1 %all-reduce.2 = f32[4]{0:T(128)S(1)} all-reduce(f32[4]{0:T(128)S(1)} %dynamic-update-slice.2), channel_id=1, replica_groups=mesh['days_0'=4,'days_1'=8,'days_2'=4,'cols'=2] {'days_2'}, use_global_device_ids=true, to_apply=%add.2 | all-reduce | flops 4 | bytes 32
  304.3 0.6 reduce_sum.49
  305.6 4.7 %broadcast_divide_fusion = f32[32,32768]{1,0:T(8,128)} fusion(f32[]{:T(128)S(6)} %sqrt.3, f32[32,32768]{1,0:T(8,128)} %copy-done, f32[32768]{0:T(1024)S(1)} %bitcast.23, pred[32]{0:T(512)(128)(4,1)S(1)} %broadcast_compare_fusion), kind=kLoop, calls=%fused_computation.10 | loop fusion | flops 3145728 | bytes 8519716 | tf_op jit(solution)/shard_map/div | solution.py:88
  310.2 0.6 dynamic-slice_divide_fusion
  (15 shorter events, 0.0 us)
Async XLA Ops:
  7.2 162.8 %all-gather.3.cloned.1.call-start = ((), (), s32[]{:S(2)}) async-start(), calls=%async_computation.1 | async-start | bytes 16974336 | tf_op jit(solution)/shard_map/all_gather | solution.py:17
  8.5 8.3 %copy-start.5 = (u32[256]{0:T(256)S(1)}, u32[256]{0:T(256)}, u32[]{:S(2)}) copy-start(u32[256]{0:T(256)} %constant.66) | copy-start | bytes 3076
  8.5 9.0 %copy-start.4 = (u32[256]{0:T(256)S(1)}, u32[256]{0:T(256)}, u32[]{:S(2)}) copy-start(u32[256]{0:T(256)} %constant.71) | copy-start | bytes 3076
  8.5 9.5 %copy-start.3 = (u32[256]{0:T(256)S(1)}, u32[256]{0:T(256)}, u32[]{:S(2)}) copy-start(u32[256]{0:T(256)} %constant.76) | copy-start | bytes 3076
  8.5 10.1 %copy-start.2 = (s32[32]{0:T(128)S(1)}, s32[32]{0:T(128)}, u32[]{:S(2)}) copy-start(s32[32]{0:T(128)} %param.6) | copy-start | bytes 388
  13.0 2.0 copy-start
  204.6 14.8 %copy-start.1 = (f32[32,32768]{1,0:T(8,128)S(1)}, f32[32,32768]{1,0:T(8,128)}, u32[]{:S(2)}) copy-start(f32[32,32768]{1,0:T(8,128)} %copy-done) | copy-start | bytes 12582916
Sparse Core Ops, SparseCore 0:
  16.9 152.9 all-gather.2
